TPU v7x, 32 devices: a whole 2x2x4 slice. The times are simulated.
32 devices in a mesh: dp: 8 (over y, x, core), mp: 4 (over z).
Axes of the slice: x: 2, y: 2, z: 4, core: 2. Of those that a mesh axis runs over, the one named last changes fastest.
Arguments:
- tokens: bfloat16 [8192, 2048], P('dp'), may hold values from -6 to 6
- doc_ids: int32 [16, 512], P('dp'), may hold values from 0 to 3, never falling along the last dimension, each value on 1 to 256 neighbouring positions
- selection: int32 [16, 512], P('dp'), may hold values 0 or 1
- w_query: bfloat16 [2048, 2048], P('dp', 'mp'), may hold values from -0.125 to 0.125
- w_key: bfloat16 [2048, 256], P('dp', 'mp'), may hold values from -0.125 to 0.125
- w_value: bfloat16 [2048, 256], P('dp', 'mp'), may hold values from -0.125 to 0.125
- w_out: bfloat16 [2048, 2048], P('mp', 'dp'), may hold values from -0.375 to 0.375
- w_gate: bfloat16 [2048, 5632], P('dp', 'mp'), may hold values from -0.125 to 0.125
- w_up: bfloat16 [2048, 5632], P('dp', 'mp'), may hold values from -0.125 to 0.125
- w_down: bfloat16 [5632, 2048], P('mp', 'dp'), may hold values from -0.078125 to 0.078125
- attn_gain: bfloat16 [2048], P('dp'), may hold values from 0.25 to 1.75
- mlp_gain: bfloat16 [2048], P('dp'), may hold values from 0.25 to 1.75
- cotangent: bfloat16 [8192, 2048], P('dp'), may hold values from -6 to 6
Outputs:
- output: bfloat16 [8192, 2048], P('dp')
- input_grad: float32 [8192, 2048], P('dp')
- grad_w_query: float32 [2048, 2048], P('dp', 'mp')
- grad_w_key: float32 [2048, 256], P('dp', 'mp')
- grad_w_value: float32 [2048, 256], P('dp', 'mp')
- grad_w_out: float32 [2048, 2048], P('mp', 'dp')
- grad_w_gate: float32 [2048, 5632], P('dp', 'mp')
- grad_w_up: float32 [2048, 5632], P('dp', 'mp')
- grad_w_down: float32 [5632, 2048], P('mp', 'dp')
- grad_attn_gain: float32 [2048], P('dp')
- grad_mlp_gain: float32 [2048], P('dp')
Inputs may be any that keep to these rules, and one draw needn't show every extreme that they name: `doc_ids`: within a sequence the ids never fall; a document spans 1 to 256 tokens and one spans exactly 256.
All inputs are finite; a program needn't handle non-finite values. No bound on the sum of `selection` on one device may be relied on, other than what follows from the above.
Results may differ from a plain program's by a relative error of at most 0.024.
Values may be sent and summed in bfloat16 or wider, within the bound.
A program may use at most 256 MiB of HBM per device.

v0:
```python
import jax
import jax.numpy as jnp
from jax import lax
from jax.sharding import PartitionSpec as P

HEAD_DIM = 64
EPSILON = 1e-05
MASKED = -1e30


def rope_tables(length, head_width):
    half_width = head_width // 2
    frequency = 10000.0 ** (-2.0 * jnp.arange(half_width, dtype=jnp.float32) / head_width)
    places = jnp.arange(length, dtype=jnp.float32)
    angles = places[:, None] * frequency[None, :]
    return (jnp.cos(angles)[:, None, :], jnp.sin(angles)[:, None, :])


def rotate(field, cosine_table, sine_table):
    half_width = field.shape[-1] // 2
    first_half = field[..., :half_width]
    second_half = field[..., half_width:]
    return jnp.concatenate(
        [
            first_half * cosine_table - second_half * sine_table,
            second_half * cosine_table + first_half * sine_table,
        ],
        axis=-1,
    )


def allowed_pairs(doc_row):
    length = doc_row.shape[0]
    query_index = lax.broadcasted_iota(jnp.int32, (length, length), 0)
    key_index = lax.broadcasted_iota(jnp.int32, (length, length), 1)
    return (doc_row[:, None] == doc_row[None, :]) & (query_index >= key_index)


def rms_forward(residual, gain_row):
    inverse = lax.rsqrt(jnp.mean(residual * residual, axis=-1, keepdims=True) + EPSILON)
    return (residual * inverse * gain_row, inverse)


def rms_backward(residual, inverse, gain_row, grad_normed):
    scaled = grad_normed * gain_row
    gain_part = jnp.sum(grad_normed * residual * inverse, axis=0)
    mean_term = jnp.mean(scaled * residual, axis=-1, keepdims=True)
    return (inverse * scaled - residual * (inverse * inverse * inverse) * mean_term, gain_part)


def attend_forward(queries, key_rows, value_rows, doc_row, score_scale):
    length, kv_local, head_width = key_rows.shape
    grouped = queries.reshape(length, kv_local, -1, head_width)
    scores = (
        jnp.einsum("qkgd,skd->kgqs", grouped, key_rows, preferred_element_type=jnp.float32)
        * score_scale
    )
    scores = jnp.where(allowed_pairs(doc_row), scores, MASKED)
    highest = jnp.max(scores, axis=-1, keepdims=True)
    shifted_exp = jnp.exp(scores - highest)
    totals = jnp.sum(shifted_exp, axis=-1, keepdims=True)
    probs_low = (shifted_exp / totals).astype(jnp.bfloat16)
    mixed_heads = jnp.einsum(
        "kgqs,skd->qkgd", probs_low, value_rows, preferred_element_type=jnp.float32
    )
    return (mixed_heads.reshape(length, -1), highest + jnp.log(totals))


def attend_backward(queries, key_rows, value_rows, doc_row, logsum, grad_mixed, score_scale):
    length, kv_local, head_width = key_rows.shape
    grouped = queries.reshape(length, kv_local, -1, head_width)
    grad_grouped = grad_mixed.reshape(length, kv_local, -1, head_width)
    scores = (
        jnp.einsum("qkgd,skd->kgqs", grouped, key_rows, preferred_element_type=jnp.float32)
        * score_scale
    )
    attn_probs = jnp.where(allowed_pairs(doc_row), jnp.exp(scores - logsum), 0.0)
    grad_probs = jnp.einsum(
        "qkgd,skd->kgqs", grad_grouped, value_rows, preferred_element_type=jnp.float32
    )
    inner_sum = jnp.sum(attn_probs * grad_probs, axis=-1, keepdims=True)
    grad_scores = (attn_probs * (grad_probs - inner_sum)).astype(jnp.bfloat16)
    grad_queries = (
        jnp.einsum("kgqs,skd->qkgd", grad_scores, key_rows, preferred_element_type=jnp.float32)
        * score_scale
    )
    grad_keys = (
        jnp.einsum("kgqs,qkgd->skd", grad_scores, grouped, preferred_element_type=jnp.float32)
        * score_scale
    )
    grad_values = jnp.einsum(
        "kgqs,qkgd->skd",
        attn_probs.astype(jnp.bfloat16),
        grad_grouped,
        preferred_element_type=jnp.float32,
    )
    return (grad_queries.reshape(length, -1, head_width), grad_keys, grad_values)


def per_device(
    tokens,
    doc_ids,
    selection,
    w_query,
    w_key,
    w_value,
    w_out,
    w_gate,
    w_up,
    w_down,
    attn_gain,
    mlp_gain,
    cotangent,
):
    (
        full_query,
        full_key,
        full_value,
        full_out,
        full_gate,
        full_up,
        full_down,
        gathered_one,
        gathered_two,
    ) = (
        lax.all_gather(w_query, "dp", axis=0, tiled=True),
        lax.all_gather(w_key, "dp", axis=0, tiled=True),
        lax.all_gather(w_value, "dp", axis=0, tiled=True),
        lax.all_gather(w_out, "dp", axis=1, tiled=True),
        lax.all_gather(w_gate, "dp", axis=0, tiled=True),
        lax.all_gather(w_up, "dp", axis=0, tiled=True),
        lax.all_gather(w_down, "dp", axis=1, tiled=True),
        lax.all_gather(attn_gain, "dp", axis=0, tiled=True),
        lax.all_gather(mlp_gain, "dp", axis=0, tiled=True),
    )
    gain_one = gathered_one.astype(jnp.float32)
    gain_two = gathered_two.astype(jnp.float32)
    seq_local, length = doc_ids.shape
    tok_local = seq_local * length
    heads_local = full_query.shape[1] // HEAD_DIM
    kv_local = full_key.shape[1] // HEAD_DIM
    score_scale = HEAD_DIM ** (-0.5)
    cosine_table, sine_table = rope_tables(length, HEAD_DIM)
    residual = tokens.astype(jnp.float32)
    normed_float, inverse_one = rms_forward(residual, gain_one)
    normed_one = normed_float.astype(jnp.bfloat16)
    query_lin = jnp.dot(normed_one, full_query, preferred_element_type=jnp.float32).reshape(
        seq_local, length, heads_local, HEAD_DIM
    )
    key_lin = jnp.dot(normed_one, full_key, preferred_element_type=jnp.float32).reshape(
        seq_local, length, kv_local, HEAD_DIM
    )
    value_rows = (
        jnp.dot(normed_one, full_value, preferred_element_type=jnp.float32)
        .astype(jnp.bfloat16)
        .reshape(seq_local, length, kv_local, HEAD_DIM)
    )
    query_rot = rotate(query_lin, cosine_table, sine_table).astype(jnp.bfloat16)
    key_rot = rotate(key_lin, cosine_table, sine_table).astype(jnp.bfloat16)

    def forward_one(bundle):
        return attend_forward(bundle[0], bundle[1], bundle[2], bundle[3], score_scale)

    mixed_heads, logsum = lax.map(forward_one, (query_rot, key_rot, value_rows, doc_ids))
    mixed_low = mixed_heads.reshape(tok_local, heads_local * HEAD_DIM).astype(jnp.bfloat16)
    attn_partial = jnp.dot(mixed_low, full_out, preferred_element_type=jnp.float32)
    hidden_in = residual + lax.psum(attn_partial.astype(jnp.bfloat16), "mp").astype(jnp.float32)
    normed_two_float, inverse_two = rms_forward(hidden_in, gain_two)
    normed_two = normed_two_float.astype(jnp.bfloat16)
    gate_lin = jnp.dot(normed_two, full_gate, preferred_element_type=jnp.float32)
    up_lin = jnp.dot(normed_two, full_up, preferred_element_type=jnp.float32)
    sig_gate = jax.nn.sigmoid(gate_lin)
    swish_gate = gate_lin * sig_gate
    hidden = (swish_gate * up_lin).astype(jnp.bfloat16)
    mlp_partial = jnp.dot(hidden, full_down, preferred_element_type=jnp.float32)
    output = (
        hidden_in + lax.psum(mlp_partial.astype(jnp.bfloat16), "mp").astype(jnp.float32)
    ).astype(jnp.bfloat16)
    grad_y = cotangent.astype(jnp.float32) * selection.reshape(tok_local, 1).astype(jnp.float32)
    grad_y_low = grad_y.astype(jnp.bfloat16)
    grad_down = jnp.einsum("tf,td->fd", hidden, grad_y_low, preferred_element_type=jnp.float32)
    grad_hidden = jnp.einsum("td,fd->tf", grad_y_low, full_down, preferred_element_type=jnp.float32)
    grad_gate_low = (grad_hidden * up_lin * sig_gate * (1.0 + gate_lin * (1.0 - sig_gate))).astype(
        jnp.bfloat16
    )
    grad_up_low = (grad_hidden * swish_gate).astype(jnp.bfloat16)
    grad_gate_w = jnp.einsum(
        "td,tf->df", normed_two, grad_gate_low, preferred_element_type=jnp.float32
    )
    grad_up_w = jnp.einsum("td,tf->df", normed_two, grad_up_low, preferred_element_type=jnp.float32)
    partial_two = jnp.einsum(
        "tf,df->td", grad_gate_low, full_gate, preferred_element_type=jnp.float32
    ) + jnp.einsum("tf,df->td", grad_up_low, full_up, preferred_element_type=jnp.float32)
    grad_normed_two = lax.psum(partial_two.astype(jnp.bfloat16), "mp").astype(jnp.float32)
    grad_resid_two, gain_grad_two = rms_backward(hidden_in, inverse_two, gain_two, grad_normed_two)
    grad_h = grad_y + grad_resid_two
    grad_h_low = grad_h.astype(jnp.bfloat16)
    grad_out_w = jnp.einsum("tc,td->cd", mixed_low, grad_h_low, preferred_element_type=jnp.float32)
    grad_mixed = jnp.einsum(
        "td,cd->tc", grad_h_low, full_out, preferred_element_type=jnp.float32
    ).astype(jnp.bfloat16)
    grad_mixed = grad_mixed.reshape(seq_local, length, heads_local * HEAD_DIM)

    def backward_one(bundle):
        return attend_backward(
            bundle[0], bundle[1], bundle[2], bundle[3], bundle[4], bundle[5], score_scale
        )

    grad_query_rot, grad_key_rot, grad_values = lax.map(
        backward_one, (query_rot, key_rot, value_rows, doc_ids, logsum, grad_mixed)
    )
    grad_query_lin = (
        rotate(grad_query_rot, cosine_table, -sine_table)
        .reshape(tok_local, heads_local * HEAD_DIM)
        .astype(jnp.bfloat16)
    )
    grad_key_lin = (
        rotate(grad_key_rot, cosine_table, -sine_table)
        .reshape(tok_local, kv_local * HEAD_DIM)
        .astype(jnp.bfloat16)
    )
    grad_value_low = grad_values.reshape(tok_local, kv_local * HEAD_DIM).astype(jnp.bfloat16)
    grad_query_w = jnp.einsum(
        "td,tc->dc", normed_one, grad_query_lin, preferred_element_type=jnp.float32
    )
    grad_key_w = jnp.einsum(
        "td,tc->dc", normed_one, grad_key_lin, preferred_element_type=jnp.float32
    )
    grad_value_w = jnp.einsum(
        "td,tc->dc", normed_one, grad_value_low, preferred_element_type=jnp.float32
    )
    partial_one = (
        jnp.einsum("tc,dc->td", grad_query_lin, full_query, preferred_element_type=jnp.float32)
        + jnp.einsum("tc,dc->td", grad_key_lin, full_key, preferred_element_type=jnp.float32)
        + jnp.einsum("tc,dc->td", grad_value_low, full_value, preferred_element_type=jnp.float32)
    )
    grad_normed_one = lax.psum(partial_one.astype(jnp.bfloat16), "mp").astype(jnp.float32)
    grad_resid_one, gain_grad_one = rms_backward(residual, inverse_one, gain_one, grad_normed_one)
    input_grad = grad_h + grad_resid_one
    (
        shard_query,
        shard_key,
        shard_value,
        shard_out,
        shard_gate,
        shard_up,
        shard_down,
        shard_gain_one,
        shard_gain_two,
    ) = (
        lax.psum_scatter(
            grad_query_w.astype(jnp.bfloat16), "dp", scatter_dimension=0, tiled=True
        ).astype(jnp.float32),
        lax.psum_scatter(
            grad_key_w.astype(jnp.bfloat16), "dp", scatter_dimension=0, tiled=True
        ).astype(jnp.float32),
        lax.psum_scatter(
            grad_value_w.astype(jnp.bfloat16), "dp", scatter_dimension=0, tiled=True
        ).astype(jnp.float32),
        lax.psum_scatter(
            grad_out_w.astype(jnp.bfloat16), "dp", scatter_dimension=1, tiled=True
        ).astype(jnp.float32),
        lax.psum_scatter(
            grad_gate_w.astype(jnp.bfloat16), "dp", scatter_dimension=0, tiled=True
        ).astype(jnp.float32),
        lax.psum_scatter(
            grad_up_w.astype(jnp.bfloat16), "dp", scatter_dimension=0, tiled=True
        ).astype(jnp.float32),
        lax.psum_scatter(
            grad_down.astype(jnp.bfloat16), "dp", scatter_dimension=1, tiled=True
        ).astype(jnp.float32),
        lax.psum_scatter(
            gain_grad_one.astype(jnp.bfloat16), "dp", scatter_dimension=0, tiled=True
        ).astype(jnp.float32),
        lax.psum_scatter(
            gain_grad_two.astype(jnp.bfloat16), "dp", scatter_dimension=0, tiled=True
        ).astype(jnp.float32),
    )
    return (
        output,
        input_grad,
        shard_query,
        shard_key,
        shard_value,
        shard_out,
        shard_gate,
        shard_up,
        shard_down,
        shard_gain_one,
        shard_gain_two,
    )


def solution(mesh):
    in_specs = (
        P("dp", None),
        P("dp", None),
        P("dp", None),
        P("dp", "mp"),
        P("dp", "mp"),
        P("dp", "mp"),
        P("mp", "dp"),
        P("dp", "mp"),
        P("dp", "mp"),
        P("mp", "dp"),
        P("dp"),
        P("dp"),
        P("dp", None),
    )
    out_specs = (
        P("dp", None),
        P("dp", None),
        P("dp", "mp"),
        P("dp", "mp"),
        P("dp", "mp"),
        P("mp", "dp"),
        P("dp", "mp"),
        P("dp", "mp"),
        P("mp", "dp"),
        P("dp"),
        P("dp"),
    )
    return jax.shard_map(
        per_device, mesh=mesh, in_specs=in_specs, out_specs=out_specs, check_vma=False
    )
```

profile of v0, /device:TPU:0, one launch (start us, length us, event | category | flops | bytes accessed | tf_op | source)
XLA Modules:
  0.0 1349.3 jit_solution(685220449423602048)
XLA Ops:
  68.6 15.0 %while.26 = (s32[]{:T(128)}, bf16[2,512,512]{2,1,0:T(8,128)(2,1)S(1)}, f32[2,1,8,512,1]{3,2,4,1,0:T(8,128)}, bf16[2,512,1,64]{1,3,2,0:T(8,128)(2,1)S(1)}, s32[2,...) while((s32[]{:T(128)}, ...), condition=%wide.region_4.5_spmd, body=%wide.region_1.4_spmd.sunk | while | flops 562819072 | bytes 29629548 | solution.py:164
  100.7 144.7 %all-reduce.8.cloned.1.call-done = bf16[1024,2048]{1,0:T(8,128)(2,1)} async-done(((bf16[1024,2048]{1,0:T(8,128)(2,1)}), bf16[1024,2048]{1,0:T(8,128)(2,1)}) %all-reduce.8.cloned.1.call-update) | async-done | bytes 4194320 | tf_op jit(solution)/shard_map/psum | solution.py:167
  255.4 34.0 %all-gather.14.cloned.1.call-done = bf16[2048,1408]{1,0:T(8,128)(2,1)} async-done(((bf16[256,1408]{1,0:T(8,128)(2,1)}), bf16[2048,1408]{1,0:T(8,128)(2,1)}) %all-gather.14.cloned.1.call-update) | async-done | bytes 5767184 | tf_op jit(solution)/shard_map/all_gather | solution.py:131
  289.3 11.7 fusion.91
  301.0 33.3 %all-gather.12.cloned.1.call-done = bf16[2048,1408]{1,0:T(8,128)(2,1)} async-done(((bf16[256,1408]{1,0:T(8,128)(2,1)}), bf16[2048,1408]{1,0:T(8,128)(2,1)}) %all-gather.12.cloned.1.call-update) | async-done | bytes 5767184 | tf_op jit(solution)/shard_map/all_gather | solution.py:130
  334.3 11.7 fusion.90
  346.0 34.3 %all-gather.16.cloned.1.call-done = bf16[1408,2048]{1,0:T(8,128)(2,1)} async-done(((bf16[1408,256]{1,0:T(8,128)(2,1)}), bf16[1408,2048]{1,0:T(8,128)(2,1)}) %all-gather.16.cloned.1.call-update) | async-done | bytes 5767184 | tf_op jit(solution)/shard_map/all_gather | solution.py:132
  380.3 17.0 %multiply_convert_fusion.1 = (bf16[1024,1408]{1,0:T(8,128)(2,1)}, bf16[1024,1408]{1,0:T(8,128)(2,1)}, bf16[1024,1408]{1,0:T(8,128)(2,1)}) fusion(f32[1024,1408]{1,0:T(8,128)} %fusion.90, f32[1024,1408]{1,0:T(8,128)} %fusion.91, bf16[1408,2048]{1,0:T(8,128)(2,1)} %all-gather.16.cloned.1.call-done, bf16[1024,2048]{1,0:T(8,128)(2,1)} %param.29, ...), kind=kOutput, calls=%fused_computation.103 | convolution fusion | flops 5933498368 | bytes 30150656 | tf_op jit(solution)/shard_map/td,fd->tf/dot_general | solution.py:182
  406.0 11.0 add_convert_fusion.1
  417.1 155.1 %all-reduce.10.cloned.1.call-done = bf16[1024,2048]{1,0:T(8,128)(2,1)} async-done(((bf16[1024,2048]{1,0:T(8,128)(2,1)}), bf16[1024,2048]{1,0:T(8,128)(2,1)}) %all-reduce.10.cloned.1.call-update) | async-done | bytes 4194320 | tf_op jit(solution)/shard_map/psum | solution.py:194
  590.2 70.1 %while.27 = (s32[]{:T(128)}, f32[2,512,8,64]{1,0,3,2:T(2,128)}, f32[2,512,1,64]{1,3,2,0:T(8,128)}, bf16[2,512,1,64]{1,3,2,0:T(8,128)(2,1)}, bf16[2,512,1,64]{1,3...) while((s32[]{:T(128)}, f32[2,512,8,64]{1,0,3,2:T(2,128)}, ...), condition=%wide.region_12.13_spmd, body=%wide.region_10.12_spmd.sunk | while | flops 1374711808 | bytes 77127944 | solution.py:209
  605.9 19.6 %dynamic_update_slice.32 = f32[2,512,8,64]{1,0,3,2:T(2,128)} dynamic-update-slice(f32[2,512,8,64]{1,0,3,2:T(2,128)} %get-tuple-element.378, f32[1,512,8,64]{1,0,3,2:T(1,128)S(1)} %copy.100, s32[]{:T(128)S(6)} %copy.121, s32[]{:T(128)} %constant.66.clone.1..sunk, s32[]{:T(128)} %constant.66.clone.1..sunk, s32[]{:T(128)} %constant.66.clone.1..sunk) | dynamic-update-slice | bytes 2097156 | tf_op jit(solution)/shard_map/while/body/jit(dynamic_update_index_in_dim)/dynamic_update_slice | solution.py:209
  640.7 19.6 %dynamic_update_slice.32 = f32[2,512,8,64]{1,0,3,2:T(2,128)} dynamic-update-slice(f32[2,512,8,64]{1,0,3,2:T(2,128)} %get-tuple-element.378, f32[1,512,8,64]{1,0,3,2:T(1,128)S(1)} %copy.100, s32[]{:T(128)S(6)} %copy.121, s32[]{:T(128)} %constant.66.clone.1..sunk, s32[]{:T(128)} %constant.66.clone.1..sunk, s32[]{:T(128)} %constant.66.clone.1..sunk) | dynamic-update-slice | bytes 2097156 | tf_op jit(solution)/shard_map/while/body/jit(dynamic_update_index_in_dim)/dynamic_update_slice | solution.py:209
  688.0 11.0 convolution_convert_fusion.1
  699.1 11.0 convolution_convert_fusion.2
  721.9 10.9 convolution_convert_fusion.3
  744.7 37.6 %reduce-scatter.8.cloned.1.call-done = bf16[256,512]{1,0:T(8,128)(2,1)} async-done(((bf16[2048,512]{1,0:T(8,128)(2,1)}), bf16[256,512]{1,0:T(8,128)(2,1)}) %reduce-scatter.8.cloned.1.call-update) | async-done | bytes 262160 | tf_op jit(solution)/shard_map/reduce_scatter | solution.py:251
  784.1 42.6 %reduce-scatter.14.cloned.1.call-done = bf16[512,256]{1,0:T(8,128)(2,1)} async-done(((bf16[512,2048]{1,0:T(8,128)(2,1)}), bf16[512,256]{1,0:T(8,128)(2,1)}) %reduce-scatter.14.cloned.1.call-update) | async-done | bytes 262160 | tf_op jit(solution)/shard_map/reduce_scatter | solution.py:260
  828.6 60.6 %reduce-scatter.18.cloned.1.call-done = bf16[256,1408]{1,0:T(8,128)(2,1)} async-done(((bf16[2048,1408]{1,0:T(8,128)(2,1)}), bf16[256,1408]{1,0:T(8,128)(2,1)}) %reduce-scatter.18.cloned.1.call-update) | async-done | bytes 720912 | tf_op jit(solution)/shard_map/reduce_scatter | solution.py:266
  891.4 60.2 %reduce-scatter.16.cloned.1.call-done = bf16[256,1408]{1,0:T(8,128)(2,1)} async-done(((bf16[2048,1408]{1,0:T(8,128)(2,1)}), bf16[256,1408]{1,0:T(8,128)(2,1)}) %reduce-scatter.16.cloned.1.call-update) | async-done | bytes 720912 | tf_op jit(solution)/shard_map/reduce_scatter | solution.py:263
  954.0 59.9 %reduce-scatter.20.cloned.1.call-done = bf16[1408,256]{1,0:T(8,128)(2,1)} async-done(((bf16[1408,2048]{1,0:T(8,128)(2,1)}), bf16[1408,256]{1,0:T(8,128)(2,1)}) %reduce-scatter.20.cloned.1.call-update) | async-done | bytes 720912 | tf_op jit(solution)/shard_map/reduce_scatter | solution.py:269
  1016.2 291.6 %all-reduce.12.cloned.1.call-done = (bf16[1024,2048]{1,0:T(8,128)(2,1)}, bf16[1024,2048]{1,0:T(8,128)(2,1)}) async-done(((bf16[1024,2048]{1,0:T(8,128)(2,1)}, bf16[1024,2048]{1,0:T(8,128)(2,1)}), (bf16[1024,2048]{1,0:T(8,128)(2,1)}, bf16[1024,2048]{1,0:T(8,128)(2,1)})) %all-reduce.12.cloned.1.call-update) | async-done | bytes 8388624 | tf_op jit(solution)/shard_map/psum | solution.py:177
  1313.4 13.7 %all-reduce.2 = (bf16[2048]{0:T(1024)(128)(2,1)S(1)}, bf16[2048]{0:T(1024)(128)(2,1)S(1)}) all-reduce(bf16[2048]{0:T(1024)(128)(2,1)S(1)} %get-tuple-element.161, bf16[2048]{0:T(1024)(128)(2,1)S(1)} %copy-done.24), channel_id=9, replica_groups=mesh['dp'=8,'mp'=4] {'dp'}, use_global_device_ids=true, to_apply=%region_23.24.clone | all-reduce | flops 4096 | bytes 16384
  1327.8 14.6 %fusion.60 = (f32[1024,2048]{1,0:T(8,128)}, bf16[1024,2048]{1,0:T(8,128)(2,1)}) fusion(f32[1024,2048]{1,0:T(8,128)} %copy-done.6, bf16[1024,2048]{1,0:T(8,128)(2,1)} %get-tuple-element.200, bf16[1024,2048]{1,0:T(8,128)(2,1)} %param.17, f32[1024]{0:T(1024)S(1)} %broadcast_multiply_fusion, f32[1024]{0:T(1024)S(1)} %copy-done.23, f32[2048]{0:T(1024)S(1)} %bitcast.299, ...), kind=kLoop, calls=%fused_computation.80 | loop fusion | flops 27262976 | bytes 37769216 | tf_op jit(solution)/shard_map/add | solution.py:239
  (220 shorter events, 227.5 us)
Async XLA Ops:
  7.2 46.4 %all-gather.8.cloned.1.call-start = ((), (), s32[]{:S(2)}) async-start(), calls=%async_computation.7 | async-start | bytes 2359296 | tf_op jit(solution)/shard_map/all_gather | solution.py:126
  7.9 75.8 %all-gather.10.cloned.1.call-start = ((), (), s32[]{:S(2)}) async-start(), calls=%async_computation.8 | async-start | bytes 2359296 | tf_op jit(solution)/shard_map/all_gather | solution.py:129
  8.7 236.7 %all-reduce.8.cloned.1.call-start = ((), (), s32[]{:S(2)}) async-start(), calls=%async_computation.9 | async-start | bytes 8388608 | tf_op jit(solution)/shard_map/psum | solution.py:167
  8.7 36.2 %copy-start = (bf16[1024,2048]{1,0:T(8,128)(2,1)S(1)}, bf16[1024,2048]{1,0:T(8,128)(2,1)}, u32[]{:S(2)}) copy-start(bf16[1024,2048]{1,0:T(8,128)(2,1)} %param.17) | copy-start | bytes 12582916
  13.4 32.6 %copy-start.21 = (f32[1024]{0:T(1024)}, f32[1024]{0:T(1024)S(1)}, u32[]{:S(2)}) copy-start(f32[1024]{0:T(1024)S(1)} %get-tuple-element.221) | copy-start | bytes 12292
  23.8 22.1 %copy-start.19 = (f32[8,1,256]{2,1,0:T(1,128)}, f32[8,1,256]{2,1,0:T(1,128)S(1)}, u32[]{:S(2)}) copy-start(f32[8,1,256]{2,1,0:T(1,128)S(1)} %convert_element_type.218) | copy-start | bytes 24580
  24.8 39.6 %copy-start.12 = (f32[512,32]{0,1:T(8,128)}, f32[512,32]{0,1:T(8,128)S(1)}, u32[]{:S(2)}) copy-start(f32[512,32]{0,1:T(8,128)S(1)} %get-tuple-element.226) | copy-start | bytes 196612
  90.1 199.3 %all-gather.14.cloned.1.call-start = ((), (), s32[]{:S(2)}) async-start(), calls=%async_computation.11 | async-start | bytes 6488064 | tf_op jit(solution)/shard_map/all_gather | solution.py:131
  90.6 243.6 %all-gather.12.cloned.1.call-start = ((), (), s32[]{:S(2)}) async-start(), calls=%async_computation.10 | async-start | bytes 6488064 | tf_op jit(solution)/shard_map/all_gather | solution.py:130
  91.2 289.1 %all-gather.16.cloned.1.call-start = ((), (), s32[]{:S(2)}) async-start(), calls=%async_computation.12 | async-start | bytes 6488064 | tf_op jit(solution)/shard_map/all_gather | solution.py:132
  91.8 480.3 %all-reduce.10.cloned.1.call-start = ((), (), s32[]{:S(2)}) async-start(), calls=%async_computation.13 | async-start | bytes 8388608 | tf_op jit(solution)/shard_map/psum | solution.py:194
  91.9 488.8 %copy-start.25 = (f32[1,4,2,128]{3,1,2,0:T(4,128)}, f32[1,4,2,128]{3,1,2,0:T(4,128)S(1)}, u32[]{:S(2)}) copy-start(f32[1,4,2,128]{3,1,2,0:T(4,128)S(1)} %copy.87) | copy-start | bytes 12292
  417.0 324.9 %reduce-scatter.10.cloned.1.call-start = ((), (), s32[]{:S(2)}) async-start(), calls=%async_computation.15 | async-start | bytes 294912 | tf_op jit(solution)/shard_map/reduce_scatter | solution.py:254
  668.0 75.3 %reduce-scatter.12.cloned.1.call-start = ((), (), s32[]{:S(2)}) async-start(), calls=%async_computation.16 | async-start | bytes 294912 | tf_op jit(solution)/shard_map/reduce_scatter | solution.py:257
  674.7 107.7 %reduce-scatter.8.cloned.1.call-start = ((), (), s32[]{:S(2)}) async-start(), calls=%async_computation.14 | async-start | bytes 2359296 | tf_op jit(solution)/shard_map/reduce_scatter | solution.py:251
  680.8 146.0 %reduce-scatter.14.cloned.1.call-start = ((), (), s32[]{:S(2)}) async-start(), calls=%async_computation.17 | async-start | bytes 2359296 | tf_op jit(solution)/shard_map/reduce_scatter | solution.py:260
  687.9 201.2 %reduce-scatter.18.cloned.1.call-start = ((), (), s32[]{:S(2)}) async-start(), calls=%async_computation.19 | async-start | bytes 6488064 | tf_op jit(solution)/shard_map/reduce_scatter | solution.py:266
  699.0 252.6 %reduce-scatter.16.cloned.1.call-start = ((), (), s32[]{:S(2)}) async-start(), calls=%async_computation.18 | async-start | bytes 6488064 | tf_op jit(solution)/shard_map/reduce_scatter | solution.py:263
  710.1 303.8 %reduce-scatter.20.cloned.1.call-start = ((), (), s32[]{:S(2)}) async-start(), calls=%async_computation.20 | async-start | bytes 6488064 | tf_op jit(solution)/shard_map/reduce_scatter | solution.py:269
  721.6 586.1 %all-reduce.12.cloned.1.call-start = ((), (), s32[]{:S(2)}) async-start(), calls=%async_computation.21 | async-start | bytes 16777216 | tf_op jit(solution)/shard_map/psum | solution.py:177
  740.0 567.7 %copy-start.20 = (f32[8,1,256]{2,1,0:T(1,128)S(1)}, f32[8,1,256]{2,1,0:T(1,128)}, u32[]{:S(2)}) copy-start(f32[8,1,256]{2,1,0:T(1,128)} %copy-done.19) | copy-start | bytes 24580
  740.0 567.7 %copy-start.22 = (f32[1024]{0:T(1024)S(1)}, f32[1024]{0:T(1024)}, u32[]{:S(2)}) copy-start(f32[1024]{0:T(1024)} %copy-done.21) | copy-start | bytes 12292
  953.9 359.5 %copy-start.24 = (bf16[2048]{0:T(1024)(128)(2,1)S(1)}, bf16[2048]{0:T(1024)(128)(2,1)}, u32[]{:S(2)}) copy-start(bf16[2048]{0:T(1024)(128)(2,1)} %get-tuple-element.159) | copy-start | bytes 12292
  953.9 373.8 %copy-start.23 = (f32[1024]{0:T(1024)S(1)}, f32[1024]{0:T(1024)}, u32[]{:S(2)}) copy-start(f32[1024]{0:T(1024)} %get-tuple-element.220) | copy-start | bytes 12292
  (29 other events, 139.6 us)
Sparse Core Ops, SparseCore 0:
  9.9 30.9 all-gather.7
  42.7 28.2 all-gather.9
  90.2 155.1 all-reduce.7
  247.1 42.1 all-gather.13
  291.0 43.1 all-gather.11
  336.0 44.2 all-gather.15
  417.1 154.9 all-reduce.9
  668.1 32.6 reduce-scatter.9
  704.4 33.6 reduce-scatter.11
  741.2 41.0 reduce-scatter.7
  785.6 41.1 reduce-scatter.13
  830.1 59.0 reduce-scatter.17
  892.6 59.0 reduce-scatter.15
  954.9 58.8 reduce-scatter.19
  1016.9 290.8 all-reduce.11
where the time goes:
time: 1360 us; the launch traced here: 1350 us
  waiting for transfers between devices  957 us (70%)
  matrix products  177 us (13%)
  other arithmetic  83.6 us (6%)
  local copies, waits for them, and re-layouts  61.2 us (4%)
  blocking collectives  53 us (4%)
  between operations  15.5 us (1%)
    psum x1, waiting for transfers between devices, per_device(): lax.psum(mlp_partial.astype(jnp.bfloat16), 'mp').astype(jnp.float32)  292 us
    psum x1, waiting for transfers between devices, per_device(): lax.psum(partial_two.astype(jnp.bfloat16), 'mp').astype(jnp.float32)  155 us
    psum x1, waiting for transfers between devices, per_device(): lax.psum(attn_partial.astype(jnp.bfloat16), 'mp').astype(jnp.float32)  145 us
    reduce_scatter x1, waiting for transfers between devices, per_device(): lax.psum_scatter(grad_up_w.astype(jnp.bfloat16), 'dp', scatter_dimension=...  60.6 us
    reduce_scatter x1, waiting for transfers between devices, per_device(): lax.psum_scatter(grad_gate_w.astype(jnp.bfloat16), 'dp', scatter_dimensio...  60.2 us
    reduce_scatter x1, waiting for transfers between devices, per_device(): lax.psum_scatter(grad_down.astype(jnp.bfloat16), 'dp', scatter_dimension=...  59.9 us
    reduce_scatter x1, waiting for transfers between devices, per_device(): lax.psum_scatter(grad_out_w.astype(jnp.bfloat16), 'dp', scatter_dimension...  42.6 us
    dynamic_update_slice x4, local copies, waits for them, and re-layouts, per_device(): lax.map(backward_one, (query_rot, key_rot, value_rows, doc_ids, logsum, g...  41.4 us
  transfers between devices with their start and end apart: 15, of which 11 were waited for; matrix products, arithmetic and copies ran while one was open for 12% of the time, Pallas kernels for 0%

commit v1 on v0

--- a/solution.py
+++ b/solution.py
@@ -6,6 +6,22 @@
 HEAD_DIM = 64
 EPSILON = 1e-05
 MASKED = -1e30
+
+
+def gather_around(x, axis, dim):
+    ways, here, hop = (lax.axis_size(axis), lax.axis_index(axis), x.shape[dim])
+    lengths = [n * ways if d == dim else n for d, n in enumerate(x.shape)]
+    full = lax.dynamic_update_slice_in_dim(jnp.zeros(lengths, x.dtype), x, here * hop, axis=dim)
+    going_up = going_down = x
+    for far in range(1, ways // 2 + 1):
+        going_up = lax.ppermute(going_up, axis, [(d, (d + 1) % ways) for d in range(ways)])
+        full = lax.dynamic_update_slice_in_dim(full, going_up, (here - far) % ways * hop, axis=dim)
+        if 2 * far < ways:
+            going_down = lax.ppermute(going_down, axis, [(d, (d - 1) % ways) for d in range(ways)])
+            full = lax.dynamic_update_slice_in_dim(
+                full, going_down, (here + far) % ways * hop, axis=dim
+            )
+    return full
 
 
 def rope_tables(length, head_width):
@@ -129,7 +145,7 @@
         lax.all_gather(w_out, "dp", axis=1, tiled=True),
         lax.all_gather(w_gate, "dp", axis=0, tiled=True),
         lax.all_gather(w_up, "dp", axis=0, tiled=True),
-        lax.all_gather(w_down, "dp", axis=1, tiled=True),
+        gather_around(w_down, "dp", 1),
         lax.all_gather(attn_gain, "dp", axis=0, tiled=True),
         lax.all_gather(mlp_gain, "dp", axis=0, tiled=True),
     )

time: 1360 us -> 1320 us (0.971)
  waiting for transfers between devices: 957 us -> 898 us
    psum x1, waiting for transfers between devices: 145 us -> 86.4 us  [per_device(): lax.psum(attn_partial.astype(jnp.bfloat16), 'mp').astype(jnp.float32)]
    all_gather x1 -> x0, waiting for transfers between devices: 34.3 us -> none  [per_device(): lax.all_gather(w_down, 'dp', axis=1, tiled=True)]
    ppermute x0 -> x7, waiting for transfers between devices: none -> 33.5 us  [the longest x4 18.2 us: gather_around(): lax.ppermute(going_up, axis, [(d, (d + 1) % ways) for d in range(ways)])]
  transfers between devices with their start and end apart: 15 -> 21, of which waited for: 11 -> 14; matrix products, arithmetic and copies ran while one was open for 12% -> 12% of each run, Pallas kernels for 0% -> 0%
where the time goes in v1:
time: 1320 us; the launch traced here: 1310 us
  waiting for transfers between devices  898 us (68%)
  matrix products  177 us (13%)
  other arithmetic  83.5 us (6%)
  local copies, waits for them, and re-layouts  74.8 us (6%)
  blocking collectives  56.8 us (4%)
  between operations  15.6 us (1%)
    psum x1, waiting for transfers between devices, per_device(): lax.psum(mlp_partial.astype(jnp.bfloat16), 'mp').astype(jnp.float32)  292 us
    psum x1, waiting for transfers between devices, per_device(): lax.psum(partial_two.astype(jnp.bfloat16), 'mp').astype(jnp.float32)  155 us
    psum x1, waiting for transfers between devices, per_device(): lax.psum(attn_partial.astype(jnp.bfloat16), 'mp').astype(jnp.float32)  86.4 us
    reduce_scatter x1, waiting for transfers between devices, per_device(): lax.psum_scatter(grad_up_w.astype(jnp.bfloat16), 'dp', scatter_dimension=...  60.7 us
    reduce_scatter x1, waiting for transfers between devices, per_device(): lax.psum_scatter(grad_gate_w.astype(jnp.bfloat16), 'dp', scatter_dimensio...  60.1 us
    reduce_scatter x1, waiting for transfers between devices, per_device(): lax.psum_scatter(grad_down.astype(jnp.bfloat16), 'dp', scatter_dimension=...  60 us
    reduce_scatter x1, waiting for transfers between devices, per_device(): lax.psum_scatter(grad_out_w.astype(jnp.bfloat16), 'dp', scatter_dimension...  42.5 us
    dynamic_update_slice x4, local copies, waits for them, and re-layouts, per_device(): lax.map(backward_one, (query_rot, key_rot, value_rows, doc_ids, logsum, g...  41.2 us
  transfers between devices with their start and end apart: 21, of which 14 were waited for; matrix products, arithmetic and copies ran while one was open for 12% of the time, Pallas kernels for 0%

profile of v1, /device:TPU:0, one launch (start us, length us, event | category | flops | bytes accessed | tf_op | source)
XLA Modules:
  0.0 1314.6 jit_solution(2002294873746499841)
XLA Ops:
  69.1 15.1 %while.26 = (s32[]{:T(128)}, bf16[2,512,512]{2,1,0:T(8,128)(2,1)S(1)}, f32[2,1,8,512,1]{3,2,4,1,0:T(8,128)}, bf16[2,512,1,64]{1,3,2,0:T(8,128)(2,1)S(1)}, s32[2,...) while((s32[]{:T(128)}, ...), condition=%wide.region_4.5_spmd, body=%wide.region_1.4_spmd.sunk | while | flops 562819072 | bytes 29629548 | solution.py:180
  94.5 16.2 %collective-permute-done = bf16[1408,256]{1,0:T(8,128)(2,1)} collective-permute-done((bf16[1408,256]{1,0:T(8,128)(2,1)S(1)}, bf16[1408,256]{1,0:T(8,128)(2,1)}, u32[]{:S(2)}, u32[]{:S(2)}) %collective-permute-start) | collective-permute-done | bytes 720928 | tf_op jit(solution)/shard_map/ppermute | solution.py:17
  110.7 12.5 all-gather.1
  159.3 86.4 %all-reduce.8.cloned.1.call-done = bf16[1024,2048]{1,0:T(8,128)(2,1)} async-done(((bf16[1024,2048]{1,0:T(8,128)(2,1)}), bf16[1024,2048]{1,0:T(8,128)(2,1)}) %all-reduce.8.cloned.1.call-update) | async-done | bytes 4194320 | tf_op jit(solution)/shard_map/psum | solution.py:183
  255.6 34.0 %all-gather.13.cloned.1.call-done = bf16[2048,1408]{1,0:T(8,128)(2,1)} async-done(((bf16[256,1408]{1,0:T(8,128)(2,1)}), bf16[2048,1408]{1,0:T(8,128)(2,1)}) %all-gather.13.cloned.1.call-update) | async-done | bytes 5767184 | tf_op jit(solution)/shard_map/all_gather | solution.py:147
  289.6 11.7 fusion.91
  301.3 33.3 %all-gather.11.cloned.1.call-done = bf16[2048,1408]{1,0:T(8,128)(2,1)} async-done(((bf16[256,1408]{1,0:T(8,128)(2,1)}), bf16[2048,1408]{1,0:T(8,128)(2,1)}) %all-gather.11.cloned.1.call-update) | async-done | bytes 5767184 | tf_op jit(solution)/shard_map/all_gather | solution.py:146
  334.6 11.8 fusion.90
  346.4 14.9 %multiply_convert_fusion.1 = (bf16[1024,1408]{1,0:T(8,128)(2,1)}, bf16[1024,1408]{1,0:T(8,128)(2,1)S(1)}, bf16[1024,1408]{1,0:T(8,128)(2,1)}) fusion(f32[1024,1408]{1,0:T(8,128)} %fusion.90, f32[1024,1408]{1,0:T(8,128)} %fusion.91, bf16[1408,2048]{1,0:T(8,128)(2,1)} %constant_dynamic-update-slice_fusion.1, bf16[1024,2048]{1,0:T(8,128)(2,1)S(1)} %copy-done.8, ...), kind=kOutput, calls=%fused_computation.103 | convolution fusion | flops 5933498368 | bytes 30150656 | tf_op jit(solution)/shard_map/td,fd->tf/dot_general | solution.py:198
  371.1 11.2 add_convert_fusion.1
  382.4 155.0 %all-reduce.10.cloned.1.call-done = bf16[1024,2048]{1,0:T(8,128)(2,1)} async-done(((bf16[1024,2048]{1,0:T(8,128)(2,1)}), bf16[1024,2048]{1,0:T(8,128)(2,1)}) %all-reduce.10.cloned.1.call-update) | async-done | bytes 4194320 | tf_op jit(solution)/shard_map/psum | solution.py:210
  555.5 70.0 %while.27 = (s32[]{:T(128)}, f32[2,512,8,64]{1,0,3,2:T(2,128)}, f32[2,512,1,64]{1,3,2,0:T(8,128)}, bf16[2,512,1,64]{1,3,2,0:T(8,128)(2,1)}, bf16[2,512,1,64]{1,3...) while((s32[]{:T(128)}, f32[2,512,8,64]{1,0,3,2:T(2,128)}, ...), condition=%wide.region_12.13_spmd, body=%wide.region_10.12_spmd.sunk | while | flops 1374711808 | bytes 77127944 | solution.py:225
  571.2 19.5 %dynamic_update_slice.72 = f32[2,512,8,64]{1,0,3,2:T(2,128)} dynamic-update-slice(f32[2,512,8,64]{1,0,3,2:T(2,128)} %get-tuple-element.378, f32[1,512,8,64]{1,0,3,2:T(1,128)S(1)} %copy.100, s32[]{:T(128)S(6)} %copy.129, s32[]{:T(128)} %constant.115.clone.1..sunk, s32[]{:T(128)} %constant.115.clone.1..sunk, s32[]{:T(128)} %constant.115.clone.1..sunk) | dynamic-update-slice | bytes 2097156 | tf_op jit(solution)/shard_map/while/body/jit(dynamic_update_index_in_dim)/dynamic_update_slice | solution.py:225
  606.0 19.5 %dynamic_update_slice.72 = f32[2,512,8,64]{1,0,3,2:T(2,128)} dynamic-update-slice(f32[2,512,8,64]{1,0,3,2:T(2,128)} %get-tuple-element.378, f32[1,512,8,64]{1,0,3,2:T(1,128)S(1)} %copy.100, s32[]{:T(128)S(6)} %copy.129, s32[]{:T(128)} %constant.115.clone.1..sunk, s32[]{:T(128)} %constant.115.clone.1..sunk, s32[]{:T(128)} %constant.115.clone.1..sunk) | dynamic-update-slice | bytes 2097156 | tf_op jit(solution)/shard_map/while/body/jit(dynamic_update_index_in_dim)/dynamic_update_slice | solution.py:225
  653.2 11.0 convolution_convert_fusion.1
  664.3 11.0 convolution_convert_fusion.2
  710.0 37.7 %reduce-scatter.8.cloned.1.call-done = bf16[256,512]{1,0:T(8,128)(2,1)} async-done(((bf16[2048,512]{1,0:T(8,128)(2,1)}), bf16[256,512]{1,0:T(8,128)(2,1)}) %reduce-scatter.8.cloned.1.call-update) | async-done | bytes 262160 | tf_op jit(solution)/shard_map/reduce_scatter | solution.py:267
  749.5 42.5 %reduce-scatter.14.cloned.1.call-done = bf16[512,256]{1,0:T(8,128)(2,1)} async-done(((bf16[512,2048]{1,0:T(8,128)(2,1)}), bf16[512,256]{1,0:T(8,128)(2,1)}) %reduce-scatter.14.cloned.1.call-update) | async-done | bytes 262160 | tf_op jit(solution)/shard_map/reduce_scatter | solution.py:276
  793.7 60.7 %reduce-scatter.18.cloned.1.call-done = bf16[256,1408]{1,0:T(8,128)(2,1)} async-done(((bf16[2048,1408]{1,0:T(8,128)(2,1)}), bf16[256,1408]{1,0:T(8,128)(2,1)}) %reduce-scatter.18.cloned.1.call-update) | async-done | bytes 720912 | tf_op jit(solution)/shard_map/reduce_scatter | solution.py:282
  856.8 60.1 %reduce-scatter.16.cloned.1.call-done = bf16[256,1408]{1,0:T(8,128)(2,1)} async-done(((bf16[2048,1408]{1,0:T(8,128)(2,1)}), bf16[256,1408]{1,0:T(8,128)(2,1)}) %reduce-scatter.16.cloned.1.call-update) | async-done | bytes 720912 | tf_op jit(solution)/shard_map/reduce_scatter | solution.py:279
  919.1 60.0 %reduce-scatter.20.cloned.1.call-done = bf16[1408,256]{1,0:T(8,128)(2,1)} async-done(((bf16[1408,2048]{1,0:T(8,128)(2,1)}), bf16[1408,256]{1,0:T(8,128)(2,1)}) %reduce-scatter.20.cloned.1.call-update) | async-done | bytes 720912 | tf_op jit(solution)/shard_map/reduce_scatter | solution.py:285
  981.5 291.6 %all-reduce.12.cloned.1.call-done = (bf16[1024,2048]{1,0:T(8,128)(2,1)}, bf16[1024,2048]{1,0:T(8,128)(2,1)}) async-done(((bf16[1024,2048]{1,0:T(8,128)(2,1)}, bf16[1024,2048]{1,0:T(8,128)(2,1)}), (bf16[1024,2048]{1,0:T(8,128)(2,1)}, bf16[1024,2048]{1,0:T(8,128)(2,1)})) %all-reduce.12.cloned.1.call-update) | async-done | bytes 8388624 | tf_op jit(solution)/shard_map/psum | solution.py:193
  1278.8 13.7 %all-reduce.2 = (bf16[2048]{0:T(1024)(128)(2,1)S(1)}, bf16[2048]{0:T(1024)(128)(2,1)S(1)}) all-reduce(bf16[2048]{0:T(1024)(128)(2,1)S(1)} %get-tuple-element.161, bf16[2048]{0:T(1024)(128)(2,1)S(1)} %copy-done.28), channel_id=9, replica_groups=mesh['dp'=8,'mp'=4] {'dp'}, use_global_device_ids=true, to_apply=%region_23.24.clone | all-reduce | flops 4096 | bytes 16384
  1293.1 14.6 %fusion.60 = (f32[1024,2048]{1,0:T(8,128)}, bf16[1024,2048]{1,0:T(8,128)(2,1)}) fusion(f32[1024,2048]{1,0:T(8,128)} %copy-done.6, bf16[1024,2048]{1,0:T(8,128)(2,1)} %get-tuple-element.200, bf16[1024,2048]{1,0:T(8,128)(2,1)} %param.17, f32[1024]{0:T(1024)S(1)} %broadcast_multiply_fusion, f32[1024]{0:T(1024)S(1)} %copy-done.25, f32[2048]{0:T(1024)S(1)} %bitcast.299, ...), kind=kLoop, calls=%fused_computation.80 | loop fusion | flops 27262976 | bytes 37769216 | tf_op jit(solution)/shard_map/add | solution.py:255
  (244 shorter events, 269.4 us)
Async XLA Ops:
  7.2 46.4 %all-gather.7.cloned.1.call-start = ((), (), s32[]{:S(2)}) async-start(), calls=%async_computation.7 | async-start | bytes 2359296 | tf_op jit(solution)/shard_map/all_gather | solution.py:142
  7.9 76.3 %all-gather.9.cloned.1.call-start = ((), (), s32[]{:S(2)}) async-start(), calls=%async_computation.8 | async-start | bytes 2359296 | tf_op jit(solution)/shard_map/all_gather | solution.py:145
  8.7 237.0 %all-reduce.8.cloned.1.call-start = ((), (), s32[]{:S(2)}) async-start(), calls=%async_computation.9 | async-start | bytes 8388608 | tf_op jit(solution)/shard_map/psum | solution.py:183
  90.5 199.1 %all-gather.13.cloned.1.call-start = ((), (), s32[]{:S(2)}) async-start(), calls=%async_computation.11 | async-start | bytes 6488064 | tf_op jit(solution)/shard_map/all_gather | solution.py:147
  91.1 243.5 %all-gather.11.cloned.1.call-start = ((), (), s32[]{:S(2)}) async-start(), calls=%async_computation.10 | async-start | bytes 6488064 | tf_op jit(solution)/shard_map/all_gather | solution.py:146
  91.7 445.8 %all-reduce.10.cloned.1.call-start = ((), (), s32[]{:S(2)}) async-start(), calls=%async_computation.12 | async-start | bytes 8388608 | tf_op jit(solution)/shard_map/psum | solution.py:210
  91.8 18.9 %collective-permute-start = (bf16[1408,256]{1,0:T(8,128)(2,1)S(1)}, bf16[1408,256]{1,0:T(8,128)(2,1)}, u32[]{:S(2)}, u32[]{:S(2)}) collective-permute-start(bf16[1408,256]{1,0:T(8,128)(2,1)S(1)} %copy-done.18), channel_id=1, source_target_pairs={{0,4},{4,8},{8,12},{12,16},{16,20},{20,24},{24,28},{28,0},{1,5},{5... | collective-permute-start | bytes 2162696 | tf_op jit(solution)/shard_map/ppermute | solution.py:17
  92.1 31.1 %collective-permute-start.1 = (bf16[1408,256]{1,0:T(8,128)(2,1)S(1)}, bf16[1408,256]{1,0:T(8,128)(2,1)}, u32[]{:S(2)}, u32[]{:S(2)}) collective-permute-start(bf16[1408,256]{1,0:T(8,128)(2,1)S(1)} %copy-done.18), channel_id=1, source_target_pairs={{0,28},{4,0},{8,4},{12,8},{16,12},{20,16},{24,20},{28,24},{1,29},{... | collective-permute-start | bytes 2162696 | tf_op jit(solution)/shard_map/ppermute | solution.py:20
  110.6 19.1 %collective-permute-start.2 = (bf16[1408,256]{1,0:T(8,128)(2,1)}, bf16[1408,256]{1,0:T(8,128)(2,1)S(1)}, u32[]{:S(2)}, u32[]{:S(2)}) collective-permute-start(bf16[1408,256]{1,0:T(8,128)(2,1)} %collective-permute-done), channel_id=1, source_target_pairs={{0,4},{4,8},{8,12},{12,16},{16,20},{20,24},{24,28},{28,0},{1,5},{5... | collective-permute-start | bytes 2162696 | tf_op jit(solution)/shard_map/ppermute | solution.py:17
  110.7 435.3 %copy-start.26 = (f32[1,4,2,128]{3,1,2,0:T(4,128)}, f32[1,4,2,128]{3,1,2,0:T(4,128)S(1)}, u32[]{:S(2)}) copy-start(f32[1,4,2,128]{3,1,2,0:T(4,128)S(1)} %copy.87) | copy-start | bytes 12292
  123.3 16.0 %collective-permute-start.3 = (bf16[1408,256]{1,0:T(8,128)(2,1)}, bf16[1408,256]{1,0:T(8,128)(2,1)S(1)}, u32[]{:S(2)}, u32[]{:S(2)}) collective-permute-start(bf16[1408,256]{1,0:T(8,128)(2,1)} %collective-permute-done.1), channel_id=1, source_target_pairs={{0,28},{4,0},{8,4},{12,8},{16,12},{20,16},{24,20},{28,24},{1,29},{... | collective-permute-start | bytes 2162696 | tf_op jit(solution)/shard_map/ppermute | solution.py:20
  129.7 15.8 %collective-permute-start.4 = (bf16[1408,256]{1,0:T(8,128)(2,1)S(1)}, bf16[1408,256]{1,0:T(8,128)(2,1)S(1)}, u32[]{:S(2)}, u32[]{:S(2)}) collective-permute-start(bf16[1408,256]{1,0:T(8,128)(2,1)S(1)} %collective-permute-done.2), channel_id=1, source_target_pairs={{0,4},{4,8},{8,12},{12,16},{16,20},{20,24},{24,28},{28,0},{1,5},{5... | collective-permute-start | bytes 2162696 | tf_op jit(solution)/shard_map/ppermute | solution.py:17
  139.2 18.2 %collective-permute-start.5 = (bf16[1408,256]{1,0:T(8,128)(2,1)S(1)}, bf16[1408,256]{1,0:T(8,128)(2,1)S(1)}, u32[]{:S(2)}, u32[]{:S(2)}) collective-permute-start(bf16[1408,256]{1,0:T(8,128)(2,1)S(1)} %collective-permute-done.3), channel_id=1, source_target_pairs={{0,28},{4,0},{8,4},{12,8},{16,12},{20,16},{24,20},{28,24},{1,29},{... | collective-permute-start | bytes 2162696 | tf_op jit(solution)/shard_map/ppermute | solution.py:20
  145.5 12.9 collective-permute-start.6
  382.4 324.8 %reduce-scatter.10.cloned.1.call-start = ((), (), s32[]{:S(2)}) async-start(), calls=%async_computation.14 | async-start | bytes 294912 | tf_op jit(solution)/shard_map/reduce_scatter | solution.py:270
  633.1 75.4 %reduce-scatter.12.cloned.1.call-start = ((), (), s32[]{:S(2)}) async-start(), calls=%async_computation.15 | async-start | bytes 294912 | tf_op jit(solution)/shard_map/reduce_scatter | solution.py:273
  639.8 107.8 %reduce-scatter.8.cloned.1.call-start = ((), (), s32[]{:S(2)}) async-start(), calls=%async_computation.13 | async-start | bytes 2359296 | tf_op jit(solution)/shard_map/reduce_scatter | solution.py:267
  646.0 146.0 %reduce-scatter.14.cloned.1.call-start = ((), (), s32[]{:S(2)}) async-start(), calls=%async_computation.16 | async-start | bytes 2359296 | tf_op jit(solution)/shard_map/reduce_scatter | solution.py:276
  653.2 201.3 %reduce-scatter.18.cloned.1.call-start = ((), (), s32[]{:S(2)}) async-start(), calls=%async_computation.18 | async-start | bytes 6488064 | tf_op jit(solution)/shard_map/reduce_scatter | solution.py:282
  664.2 252.6 %reduce-scatter.16.cloned.1.call-start = ((), (), s32[]{:S(2)}) async-start(), calls=%async_computation.17 | async-start | bytes 6488064 | tf_op jit(solution)/shard_map/reduce_scatter | solution.py:279
  675.3 303.9 %reduce-scatter.20.cloned.1.call-start = ((), (), s32[]{:S(2)}) async-start(), calls=%async_computation.19 | async-start | bytes 6488064 | tf_op jit(solution)/shard_map/reduce_scatter | solution.py:285
  686.8 586.3 %all-reduce.12.cloned.1.call-start = ((), (), s32[]{:S(2)}) async-start(), calls=%async_computation.20 | async-start | bytes 16777216 | tf_op jit(solution)/shard_map/psum | solution.py:193
  705.3 567.8 %copy-start.22 = (f32[8,1,256]{2,1,0:T(1,128)S(1)}, f32[8,1,256]{2,1,0:T(1,128)}, u32[]{:S(2)}) copy-start(f32[8,1,256]{2,1,0:T(1,128)} %copy-done.21) | copy-start | bytes 24580
  705.3 567.8 %copy-start.24 = (f32[1024]{0:T(1024)S(1)}, f32[1024]{0:T(1024)}, u32[]{:S(2)}) copy-start(f32[1024]{0:T(1024)} %copy-done.23) | copy-start | bytes 12292
  (37 other events, 1054.0 us)
Sparse Core Ops, SparseCore 0:
  9.9 30.9 all-gather.6
  42.8 28.2 all-gather.8
  90.7 154.9 all-reduce.7
  247.4 42.1 all-gather.12
  291.4 43.1 all-gather.10
  382.5 154.9 all-reduce.9
  633.3 32.6 reduce-scatter.9
  669.5 33.6 reduce-scatter.11
  706.5 41.0 reduce-scatter.7
  750.8 41.1 reduce-scatter.13
  795.4 59.0 reduce-scatter.17
  857.8 59.0 reduce-scatter.15
  920.2 58.8 reduce-scatter.19
  982.2 290.8 all-reduce.11
